TPU v7x, 32 devices: a whole 2x2x4 slice. The times are simulated.
32 devices in a mesh: pts: 16 (over z, x, core), grp: 2 (over y).
Axes of the slice: x: 2, y: 2, z: 4, core: 2. Of those that a mesh axis runs over, the one named last changes fastest.
Arguments:
- cam_jac: float32 [2, 9, 219136], P(None, None, ('pts', 'grp')), may hold values from -6 to 6
- pt_jac: float32 [2, 3, 219136], P(None, None, ('pts', 'grp')), may hold values from -6 to 6
- cam_slot: int32 [219136], P(('pts', 'grp')), may hold values from 0 to 127
- obs_point: int32 [219136], P(('pts', 'grp')), may hold values from 0 to 2047
- cam_inverse: float32 [9, 9, 13696], replicated, may hold values from -1 to 1, as said below
- pt_inverse: float32 [3, 3, 65536], P(None, None, ('pts', 'grp')), may hold values from -1 to 1, as said below
- cam_rhs: float32 [9, 13696], replicated, may hold values from -48 to 48
- pt_rhs: float32 [3, 65536], P(None, ('pts', 'grp')), may hold values from -240 to 240
Outputs:
- camera_step: float32 [9, 13696], replicated
- point_step: float32 [3, 65536], P(None, ('pts', 'grp'))
- resid_ratio: float32 [], replicated
Inputs may be any that keep to these rules, and one draw needn't show every extreme that they name: The observations of each device come in 107 runs of 64; run b holds observations of cameras b * 128 to (b + 1) * 128 - 1, and cam_slot is the camera's offset in that run's block. The point of observation o is (o // 6848) * 2048 + obs_point[o]. `cam_inverse`: each camera's 9 x 9 block is symmetric positive definite. `pt_inverse`: each point's 3 x 3 block is symmetric positive definite.
All inputs are finite; a program needn't handle non-finite values.
Results may differ from a plain program's by a relative error of at most 0.00014.
Values sent between devices are 32-bit elements; how exact they have to be, the bound alone decides.
A program may use at most 128 MiB of HBM per device.

v0:
```python
import functools

import jax
import jax.numpy as jnp
from jax import lax
from jax.experimental import pallas as pl
from jax.experimental.pallas import tpu as pltpu
from jax.sharding import PartitionSpec as P

CAM_BLK = 128
TERMS = 3
PER = 4
ROWS = 40
MESH = pl.DeviceIdType.MESH
VMEM = pl.BlockSpec(memory_space=pltpu.VMEM)
F32 = jnp.float32
BF16 = jnp.bfloat16


def halves(v):
    top = v.astype(BF16)
    return top, (v - top.astype(F32)).astype(BF16)


def rows_of(group):
    return 16 * (group // 2) + group % 2


def prepare(obs, live, cj_in, pj_in, slot, point, pinv_in, prhs_in, cj, pj, pinv, prhs, tail, right, hot):
    for a in range(2):
        for ref, out, count in ((cj_in, cj, 9), (pj_in, pj, 3)):
            for j in range(count):
                begin = live // 8 * 8
                out[(a * count + j) * 64 + begin : (a * count + j + 1) * 64, :] = jnp.zeros((64 - begin, 128), F32)
    tail[...] = jnp.zeros((16, 128), F32)
    for r in range(live):
        span = min(128, obs - r * 128)
        for a in range(2):
            for ref, out, count in ((cj_in, cj, 9), (pj_in, pj, 3)):
                if span == 128:
                    v = ref[a, :, r * 128 : r * 128 + 128]
                else:
                    tail[0:count, 0:span] = ref[a, :, r * 128 : r * 128 + span]
                    v = tail[0:count, :]
                out[pl.ds(a * count * 64 + r, count, stride=64), :] = v
    for s in range(16):
        cols = slice(s * 128, s * 128 + 128)
        prhs[pl.ds(s, 3, stride=16), :] = prhs_in[:, cols]
        for i in range(3):
            pinv[pl.ds(48 * i + s, 3, stride=16), :] = pinv_in[i, :, cols]
    low = lax.broadcasted_iota(jnp.int32, (128, 128), 0)
    for r in range(live):
        cols = slice(r * 128, (r + 1) * 128)
        right[:, cols] = jnp.where(low == (point[r : r + 1, :] & 127), 1.0, 0.0).astype(BF16)
        hot[:, cols] = jnp.where(low == slot[r : r + 1, :], 1.0, 0.0).astype(BF16)


def to_points(live, groups, vec, cj, pj, slot, point, quant, left, right):
    lane_low = lax.broadcasted_iota(jnp.int32, (8, 128), 1) < 64
    for group in range(groups):
        u, half = group // 2, group % 2
        row = rows_of(group)
        index = slot[pl.ds(row, 8, stride=2), :]
        proj = [None, None]
        for j in range(9):
            even = vec[pl.ds(8 * u * ROWS + (2 * half) * 9 + j, 8, stride=ROWS), :]
            odd = vec[pl.ds(8 * u * ROWS + (2 * half + 1) * 9 + j, 8, stride=ROWS), :]
            even = jnp.take_along_axis(even, index, axis=1, mode="promise_in_bounds")
            odd = jnp.take_along_axis(odd, index, axis=1, mode="promise_in_bounds")
            got = jnp.where(lane_low, even, odd)
            for a in range(2):
                part = cj[pl.ds((a * 9 + j) * 64 + row, 8, stride=2), :] * got
                proj[a] = part if proj[a] is None else proj[a] + part
        for i in range(3):
            quant[pl.ds(64 * i + row, 8, stride=2), :] = (
                pj[pl.ds(64 * i + row, 8, stride=2), :] * proj[0]
                + pj[pl.ds(64 * (3 + i) + row, 8, stride=2), :] * proj[1]
            )
    high = lax.broadcasted_iota(jnp.int32, (16, 128), 0)
    for r in range(live):
        cols = slice(r * 128, (r + 1) * 128)
        hit = high == (point[r : r + 1, :] >> 7)
        for i in range(3):
            v = jnp.where(hit, quant[64 * i + r : 64 * i + r + 1, :], 0.0)
            top, rest = halves(v)
            left[i * 16 : i * 16 + 16, cols] = top
            left[48 + i * 16 : 64 + i * 16, cols] = rest
    both = lax.dot_general(left[...], right[...], (((1,), (1,)), ((), ())), preferred_element_type=F32)
    return both[0:48] + both[48:96]


def point_solve(pinv, y):
    out = []
    for i in range(3):
        row = 48 * i
        out.append(
            pinv[row : row + 16] * y[0:16] + pinv[row + 16 : row + 32] * y[16:32] + pinv[row + 32 : row + 48] * y[32:48]
        )
    return jnp.concatenate(out, axis=0)


def to_cameras(live, groups, z, cj, pj, slot, point, hot, pull, out):
    for group in range(groups):
        row = rows_of(group)
        where = point[pl.ds(row, 8, stride=2), :]
        low, high = where & 127, where >> 7
        got = [jnp.zeros((8, 128), F32)] * 3
        for s in range(16):
            hit = high == s
            for i in range(3):
                table = jnp.broadcast_to(z[16 * i + s : 16 * i + s + 1, :], (8, 128))
                cand = jnp.take_along_axis(table, low, axis=1, mode="promise_in_bounds")
                got[i] = jnp.where(hit, cand, got[i])
        proj = []
        for a in range(2):
            part = None
            for i in range(3):
                term = pj[pl.ds((3 * a + i) * 64 + row, 8, stride=2), :] * got[i]
                part = term if part is None else part + term
            proj.append(part)
        for j in range(9):
            pull[pl.ds(64 * j + row, 8, stride=2), :] = (
                cj[pl.ds(64 * j + row, 8, stride=2), :] * proj[0]
                + cj[pl.ds(64 * (9 + j) + row, 8, stride=2), :] * proj[1]
            )
    lane_low = lax.broadcasted_iota(jnp.int32, (16, 128), 1) < 64
    for r in range(live):
        v = pull[pl.ds(r, 16, stride=64), :]
        e_top, e_rest = halves(jnp.where(lane_low, v, 0.0))
        o_top, o_rest = halves(jnp.where(lane_low, 0.0, v))
        lhs = jnp.concatenate([e_top, e_rest, o_top, o_rest], axis=0)
        d = lax.dot_general(
            lhs, hot[:, r * 128 : r * 128 + 128], (((1,), (1,)), ((), ())), preferred_element_type=F32
        )
        base = (r // 2) * ROWS + (r % 2) * 18
        out[base : base + 9, :] = (d[0:16] + d[16:32])[0:9]
        out[base + 9 : base + 18, :] = (d[32:48] + d[48:64])[0:9]


def body(
    chips, grp_size, chunks, slots, blocks, live, groups, obs,
    cj_in, pj_in, slot, point, pinv_in, prhs_in, cinv, crhs,
    cam_out, pt_out, ratio_out,
    cj, pj, pinv, prhs, tail, right, hot, left, quant, pull, zs, x, inv, rhs, kept,
    twin_buf, mine, inbox, result, tile, pair, tiles, left_tiles,
    a_s, a_r, b_s, b_r, c_s, c_r, d_s, d_r, load, p_s, p_r, q_s, q_r,
):
    pts, grp = lax.axis_index("pts"), lax.axis_index("grp")
    core = lax.rem(pts, 2)
    chip = (pts // 2) * grp_size + grp
    twin = (pts + 1 - 2 * core, grp)

    def at(other):
        return (2 * (other // grp_size) + core, lax.rem(other, grp_size))

    def around(k):
        return lax.rem(chip + k, chips)

    def loop(start, step):
        def run(k, carry):
            step(k)
            return carry

        lax.fori_loop(start, chips, run, 0)

    barrier = pltpu.get_barrier_semaphore()
    pl.semaphore_signal(barrier, inc=1, device_id=twin, device_id_type=MESH)
    loop(1, lambda k: pl.semaphore_signal(barrier, inc=1, device_id=at(around(k)), device_id_type=MESH))

    def owned(c, t):
        return jnp.logical_and(t < slots, c * slots + t < chunks)

    def owned_block(b):
        return jnp.logical_and(chip < slots, (core * slots + chip) * PER + b < blocks)

    def loads(b):
        cols = pl.ds(pl.multiple_of(((core * slots + chip) * PER + b) * 128, 128), 128)
        return (
            pltpu.make_async_copy(cinv.at[:, :, cols], inv.at[b], load.at[2 * b]),
            pltpu.make_async_copy(crhs.at[:, cols], rhs.at[b], load.at[2 * b + 1]),
        )

    for b in range(PER):
        @pl.when(owned_block(b))
        def _():
            for copy in loads(b):
                copy.start()

        @pl.when(jnp.logical_not(owned_block(b)))
        def _():
            inv[b] = jnp.zeros((9, 9, 128), F32)
            rhs[b] = jnp.zeros((9, 128), F32)

    prepare(obs, live, cj_in, pj_in, slot, point, pinv_in, prhs_in, cj, pj, pinv, prhs, tail, right, hot)
    x[...] = jnp.zeros_like(x)
    result[...] = jnp.zeros_like(result)
    kept[...] = jnp.zeros_like(kept)
    pull[pl.ds(9 * 64, 7 * 64), :] = jnp.zeros((7 * 64, 128), F32)
    zs[...] = prhs[...]
    for b in range(PER):
        @pl.when(owned_block(b))
        def _():
            for copy in loads(b):
                copy.wait()

    pl.semaphore_wait(barrier, chips)

    def chunk(c, t):
        return pl.ds(pl.multiple_of((c * slots + t) * ROWS, 8), ROWS)

    def remote(src, dst, send, recv, device):
        return pltpu.make_async_remote_copy(
            src_ref=src, dst_ref=dst, send_sem=send, recv_sem=recv, device_id=device, device_id_type=MESH
        )

    def to_twin(t):
        return remote(x.at[chunk(1 - core, t)], twin_buf.at[t], a_s.at[t], a_r.at[t], twin)

    def to_owner(t):
        return remote(mine.at[t], inbox.at[chip], b_s.at[t], b_r.at[chip], at(t))

    def from_peer(t):
        return remote(mine.at[0], inbox.at[t], b_s.at[0], b_r.at[t], at(t))

    def spread(t):
        part = result.at[chunk(core, chip)]
        return remote(part, part, c_s.at[t], c_r.at[chip], at(t))

    def spread_in(t):
        part = result.at[chunk(core, t)]
        return remote(part, part, c_s.at[0], c_r.at[t], at(t))

    def pass_on(t):
        part = result.at[chunk(core, t)]
        return remote(part, part, d_s.at[t], d_r.at[t], twin)

    def pass_in(t):
        part = result.at[chunk(1 - core, t)]
        return remote(part, part, d_s.at[0], d_r.at[t], twin)

    def start_twin(k):
        t = around(k)
        pl.when(owned(1 - core, t))(lambda: to_twin(t).start())

    def reduce_pair(k, send):
        t = around(k)

        @pl.when(owned(core, t))
        def _():
            to_twin(t).wait_recv()
            mine[t] = x[chunk(core, t), :] + twin_buf[t]
            if send:
                to_owner(t).start()

    def forward(k):
        t = around(chips - k)

        @pl.when(owned(core, t))
        def _():
            spread_in(t).wait_recv()
            pass_on(t).start()

    def finish(k):
        t = around(k)
        pl.when(owned(1 - core, t))(lambda: pass_in(t).wait_recv())

    def drain(k):
        t = around(k)
        pl.when(owned(1 - core, t))(lambda: to_twin(t).wait_send())
        pl.when(owned(core, t))(lambda: pass_on(t).wait_send())

    def drain_peers(k):
        t = around(k)
        pl.when(owned(core, t))(lambda: to_owner(t).wait_send())
        pl.when(owned(core, chip))(lambda: spread(t).wait_send())

    def exchange(index):
        loop(1, start_twin)
        start_twin(0)
        loop(1, lambda k: reduce_pair(k, True))
        reduce_pair(0, False)

        @pl.when(owned(core, chip))
        def _():
            tile[...] = mine[chip]

            def gather(k):
                t = around(chips - k)
                from_peer(t).wait_recv()
                tile[...] += inbox[t]

            loop(1, gather)
            solved = []
            for b in range(PER):
                total = tile[9 * b : 9 * b + 9, :]
                total = jnp.where(index == 0, rhs[b] - total, total)
                piece = None
                for j in range(9):
                    term = inv[b, j] * total[j : j + 1, :]
                    piece = term if piece is None else piece + term
                solved.append(piece)
            solved = jnp.concatenate(solved + [jnp.zeros((ROWS - 9 * PER, 128), F32)], axis=0)
            step = kept[...] + solved
            kept[...] = step
            result[chunk(core, chip), :] = jnp.where(index == TERMS, step, solved)
            loop(1, lambda k: spread(around(k)).start())
            pass_on(chip).start()

        loop(1, forward)
        loop(0, finish)
        loop(0, drain)
        loop(1, drain_peers)

    def term(index, carry):
        solved = point_solve(pinv, zs[...])
        zs[...] = solved
        to_cameras(live, groups, zs, cj, pj, slot, point, hot, pull, x)
        exchange(index)
        zs[...] = to_points(live, groups, result, cj, pj, slot, point, quant, left, right)
        return carry

    lax.fori_loop(0, TERMS + 1, term, 0)
    rhs_pts = prhs[...]
    resid = rhs_pts - zs[...]
    for row, vals in ((0, resid * resid), (1, rhs_pts * rhs_pts)):
        total = vals[0:8]
        for k in range(1, 6):
            total = total + vals[8 * k : 8 * k + 8]
        tiles[8 * row : 8 * row + 8, :] = total

    def swap():
        return remote(tiles, pair, p_s, p_r, twin)

    def share(t, slot_of):
        return remote(left_tiles.at[chip], left_tiles.at[slot_of], q_s.at[t], q_r.at[slot_of], at(t))

    swap().start()
    swap().wait_recv()
    left_tiles[chip] = tiles[...] + pair[...]
    loop(1, lambda k: share(around(k), chip).start())
    zs[...] = point_solve(pinv, resid)
    for s in range(16):
        pt_out[:, s * 128 : s * 128 + 128] = zs[pl.ds(s, 3, stride=16), :]
    for b in range(blocks):
        base = (b // PER) * ROWS + (b % PER) * 9
        cam_out[:, b * 128 : b * 128 + 128] = result[base : base + 9, :]

    def collect(k):
        t = around(k)
        share(t, t).wait_recv()

    loop(1, collect)
    total = left_tiles[0]
    for t in range(1, chips):
        total = total + left_tiles[t]
    ratio_out[...] = jnp.sqrt(jnp.sum(total[0:8], keepdims=True) / jnp.sum(total[8:16], keepdims=True))
    loop(1, lambda k: share(around(k), chip).wait_send())
    swap().wait_send()


def local(pts_size, grp_size, cam_jac, pt_jac, cam_slot, obs_point, cam_inverse, pt_inverse, cam_rhs, pt_rhs):
    obs = cam_slot.shape[0]
    cameras = cam_rhs.shape[1]
    blocks = cameras // CAM_BLK
    points = pt_rhs.shape[1]
    chips = pts_size * grp_size // 2
    chunks = -(-blocks // PER)
    slots = -(-chunks // 16) * 8
    assert obs == blocks * 64 and slots <= chips and slots == 16 and points == 2048
    live = -(-obs // 128)
    groups = 2 * (-(-live // 16))

    def pad_obs(v):
        return jnp.pad(v, (0, 64 * 128 - obs)).reshape(64, 128)

    def vmem(*shape):
        return pltpu.VMEM(shape, F32)

    dma = pltpu.SemaphoreType.DMA
    anywhere = pl.BlockSpec(memory_space=pl.ANY)
    wide = live * 128
    camera_step, point_step, ratio = pl.pallas_call(
        functools.partial(body, chips, grp_size, chunks, slots, blocks, live, groups, obs),
        out_shape=(
            jax.ShapeDtypeStruct((9, cameras), F32),
            jax.ShapeDtypeStruct((3, points), F32),
            jax.ShapeDtypeStruct((1, 1), F32),
        ),
        in_specs=[VMEM] * 6 + [anywhere] * 2,
        out_specs=(VMEM, VMEM, VMEM),
        scratch_shapes=[
            vmem(18 * 64, 128), vmem(6 * 64, 128), vmem(9 * 16, 128), vmem(48, 128), vmem(16, 128),
            pltpu.VMEM((128, wide), BF16), pltpu.VMEM((128, wide), BF16), pltpu.VMEM((96, wide), BF16),
            vmem(3 * 64, 128), vmem(16 * 64, 128), vmem(48, 128), vmem(2 * slots * ROWS, 128),
            vmem(PER, 9, 9, 128), vmem(PER, 9, 128), vmem(ROWS, 128),
            vmem(slots, ROWS, 128), vmem(slots, ROWS, 128), vmem(chips, ROWS, 128), vmem(2 * slots * ROWS, 128),
            vmem(ROWS, 128), vmem(16, 128), vmem(16, 128), vmem(chips, 16, 128),
            dma((slots,)), dma((slots,)), dma((slots,)), dma((chips,)),
            dma((chips,)), dma((slots,)), dma((slots,)), dma((slots,)),
            dma((2 * PER,)), dma, dma, dma((chips,)), dma((chips,)),
        ],
        compiler_params=pltpu.CompilerParams(collective_id=0, has_side_effects=True),
        name="schur",
    )(cam_jac, pt_jac, pad_obs(cam_slot), pad_obs(obs_point), pt_inverse, pt_rhs, cam_inverse, cam_rhs)
    return camera_step, point_step, ratio.reshape(())


def solution(mesh):
    placed = (
        P(None, None, ("pts", "grp")),
        P(None, None, ("pts", "grp")),
        P(("pts", "grp")),
        P(("pts", "grp")),
        P(),
        P(None, None, ("pts", "grp")),
        P(),
        P(None, ("pts", "grp")),
    )
    return jax.shard_map(
        functools.partial(local, mesh.shape["pts"], mesh.shape["grp"]),
        mesh=mesh,
        in_specs=placed,
        out_specs=(P(), P(None, ("pts", "grp")), P()),
        check_vma=False,
    )
```

profile of v0, /device:TPU:0, one launch (start us, length us, event | category | flops | bytes accessed | tf_op | source)
XLA Modules:
  0.0 115.0 jit_solution(6004354108646725576)
XLA Ops:
  0.6 1.4 %pad_bitcast_fusion = (s32[64,128]{1,0:T(8,128)}, s32[64,128]{1,0:T(8,128)}) fusion(s32[6848]{0:T(1024)} %param.11, s32[6848]{0:T(1024)} %param.10), kind=kLoop, calls=%fused_computation | loop fusion | bytes 120320 | tf_op jit(solution)/shard_map/reshape | solution.py:374
  2.0 1.7 %copy.12.pj_in = f32[2,3,6848]{2,1,0:T(4,128)} copy(f32[2,3,6848]{2,0,1:T(2,128)} %param.9) | data formatting | bytes 328704 | tf_op args[1]
  3.7 2.0 %copy.11.cj_in = f32[2,9,6848]{2,1,0:T(8,128)} copy(f32[2,9,6848]{2,0,1:T(2,128)} %param.8) | data formatting | bytes 986112 | tf_op args[0]
  5.7 104.0 %schur.1 = (f32[9,13696]{1,0:T(8,128)}, f32[3,2048]{1,0:T(4,128)}, f32[1,1]{1,0:T(1,128)}) custom-call(f32[2,9,6848]{2,1,0:T(8,128)} %copy.11.cj_in, f32[2,3,6848]{2,1,0:T(4,128)} %copy.12.pj_in, s32[64,128]{1,0:T(8,128)} %get-tuple-element.10.slot, s32[64,128]{1,0:T(8,128)} %get-tuple-element.9.point, f32[3,3,2048]{2,1,0:T(4,128)} %pinv_in.1, ...), custom_call_target="tpu_custom_call" | custom-call | tf_op jit(solution)/shard_map/schur/pallas_call | solution.py:382
  109.7 2.1 %copy.16 = f32[9,13696]{1,0:T(8,128)} copy(f32[9,13696]{1,0:T(8,128)} %get-tuple-element.14) | data formatting | bytes 986112
  111.8 1.4 %copy.17 = f32[3,2048]{1,0:T(4,128)} copy(f32[3,2048]{1,0:T(4,128)} %get-tuple-element.15) | data formatting | bytes 49152
where the time goes:
time: 115 us
  Pallas kernels  104 us (90%)
  local copies, waits for them, and re-layouts  8.57 us (7%)
  between operations  2.46 us (2%)
    pallas_call x1, Pallas kernels, local(): pl.pallas_call(functools.partial(body, chips, grp_size, chunks, slots, bl...  104 us
    unnamed x4, local copies, waits for them, and re-layouts  7.19 us

commit v1 on v0

v1 whole, which is shorter than its diff:
```python
import functools

import jax
import jax.numpy as jnp
from jax import lax
from jax.experimental import pallas as pl
from jax.experimental.pallas import tpu as pltpu
from jax.sharding import PartitionSpec as P

CAM_BLK = 128
TERMS = 3
MESH = pl.DeviceIdType.MESH
VMEM = pl.BlockSpec(memory_space=pltpu.VMEM)
F32 = jnp.float32
BF16 = jnp.bfloat16


def halves(v):
    top = v.astype(BF16)
    return top, (v - top.astype(F32)).astype(BF16)


def prepare(obs, live, per, msg, cj_in, pj_in, slot_in, point_in, cjm, pj, slot, point):
    slot[...] = jnp.zeros_like(slot)
    point[...] = jnp.zeros_like(point)
    for r in range(live):
        span = min(128, obs - r * 128)
        cols = slice(r * 128, r * 128 + span)
        slot[r : r + 1, 0:span] = slot_in[cols].reshape(1, span)
        point[r : r + 1, 0:span] = point_in[cols].reshape(1, span)
        base = (r // per) * msg + (r % per) * 18
        for j in range(9):
            cjm[base + 2 * j : base + 2 * j + 2, 0:span] = cj_in[j, :, cols]
        for i in range(3):
            pj[(i * 64 + r) * 2 : (i * 64 + r) * 2 + 2, 0:span] = pj_in[i, :, cols]
        if span < 128:
            cjm[base : base + 18, span:128] = jnp.zeros((18, 128 - span), F32)
            for i in range(3):
                pj[(i * 64 + r) * 2 : (i * 64 + r) * 2 + 2, span:128] = jnp.zeros((2, 128 - span), F32)
    for i in range(3):
        pj[(i * 64 + live) * 2 : (i * 64 + 64) * 2, :] = jnp.zeros(((64 - live) * 2, 128), F32)


def prepare_points(live, pinv_in, prhs_in, point, pinv, prhs, right):
    for s in range(16):
        cols = slice(s * 128, s * 128 + 128)
        prhs[pl.ds(s, 3, stride=16), :] = prhs_in[:, cols]
        for i in range(3):
            pinv[pl.ds(48 * i + s, 3, stride=16), :] = pinv_in[i, :, cols]
    low = lax.broadcasted_iota(jnp.int32, (128, 128), 0)
    for r in range(live):
        cols = slice(r * 128, (r + 1) * 128)
        right[:, cols] = jnp.where(low == (point[r : r + 1, :] & 127), 1.0, 0.0).astype(BF16)


def point_solve(pinv, y):
    out = []
    for i in range(3):
        row = 48 * i
        out.append(
            pinv[row : row + 16] * y[0:16] + pinv[row + 16 : row + 32] * y[16:32] + pinv[row + 32 : row + 48] * y[32:48]
        )
    return jnp.concatenate(out, axis=0)


def from_points(groups, z, pj, point, s_out):
    for g in range(groups):
        where = point[8 * g : 8 * g + 8, :]
        low, high = where & 127, where >> 7
        got = [jnp.zeros((8, 128), F32)] * 3
        for s in range(16):
            hit = high == s
            for i in range(3):
                table = jnp.broadcast_to(z[16 * i + s : 16 * i + s + 1, :], (8, 128))
                cand = jnp.take_along_axis(table, low, axis=1, mode="promise_in_bounds")
                got[i] = jnp.where(hit, cand, got[i])
        for a in range(2):
            part = None
            for i in range(3):
                term = pj[pl.ds((i * 64 + 8 * g) * 2 + a, 8, stride=2), :] * got[i]
                part = term if part is None else part + term
            s_out[pl.ds(16 * g + a, 8, stride=2), :] = part


def onto_points(live, groups, r_in, pj, point, quant, left, right):
    for g in range(groups):
        proj = [r_in[pl.ds(16 * g + a, 8, stride=2), :] for a in range(2)]
        for i in range(3):
            quant[64 * i + 8 * g : 64 * i + 8 * g + 8, :] = (
                pj[pl.ds((i * 64 + 8 * g) * 2, 8, stride=2), :] * proj[0]
                + pj[pl.ds((i * 64 + 8 * g) * 2 + 1, 8, stride=2), :] * proj[1]
            )
    high = lax.broadcasted_iota(jnp.int32, (16, 128), 0)
    for r in range(live):
        cols = slice(r * 128, (r + 1) * 128)
        hit = high == (point[r : r + 1, :] >> 7)
        for i in range(3):
            v = jnp.where(hit, quant[64 * i + r : 64 * i + r + 1, :], 0.0)
            top, rest = halves(v)
            left[i * 16 : i * 16 + 16, cols] = top
            left[48 + i * 16 : 64 + i * 16, cols] = rest
    both = lax.dot_general(left[...], right[...], (((1,), (1,)), ((), ())), preferred_element_type=F32)
    return both[0:48] + both[48:96]


def build_hot(n, per, slots, hot):
    low = lax.broadcasted_iota(jnp.int32, (128, 128), 0)
    for src in range(n):
        for p in range(per):
            row = src * per + p
            hot[p, :, src * 128 : src * 128 + 128] = jnp.where(low == slots[row : row + 1, :], 1.0, 0.0).astype(BF16)


def gather_blocks(n, per, msg, s_in, cjo, hot, pull, lhs):
    width = 2 * per
    for g in range(n // 8):
        for p in range(per):
            s = [s_in[pl.ds(8 * g * width + 2 * p + a, 8, stride=width), :] for a in range(2)]
            for j in range(9):
                at = 8 * g * msg + p * 18 + 2 * j
                pull[pl.ds((8 * g * per + p) * 16 + j, 8, stride=16 * per), :] = (
                    cjo[pl.ds(at, 8, stride=msg), :] * s[0] + cjo[pl.ds(at + 1, 8, stride=msg), :] * s[1]
                )
    lane_low = lax.broadcasted_iota(jnp.int32, (16, 128), 1) < 64
    sums = []
    for p in range(per):
        for src in range(n):
            cols = slice(src * 128, src * 128 + 128)
            base = (src * per + p) * 16
            v = pull[base : base + 16, :]
            e_top, e_rest = halves(jnp.where(lane_low, v, 0.0))
            o_top, o_rest = halves(jnp.where(lane_low, 0.0, v))
            for k, piece in enumerate((e_top, e_rest, o_top, o_rest)):
                lhs[p, 16 * k : 16 * k + 16, cols] = piece
        d = lax.dot_general(lhs[p], hot[p], (((1,), (1,)), ((), ())), preferred_element_type=F32)
        sums.append((d[0:16] + d[16:32])[0:9])
        sums.append((d[32:48] + d[48:64])[0:9])
    return sums


def spread_blocks(n, per, msg, xs, slots, cjo, r_out):
    width = 2 * per
    lane_low = lax.broadcasted_iota(jnp.int32, (8, 128), 1) < 64
    for g in range(n // 8):
        for p in range(per):
            index = slots[pl.ds(8 * g * per + p, 8, stride=per), :]
            proj = [None, None]
            for j in range(9):
                row = 32 * p + j
                even = jnp.broadcast_to(xs[row : row + 1, :], (8, 128))
                odd = jnp.broadcast_to(xs[row + 16 : row + 17, :], (8, 128))
                even = jnp.take_along_axis(even, index, axis=1, mode="promise_in_bounds")
                odd = jnp.take_along_axis(odd, index, axis=1, mode="promise_in_bounds")
                got = jnp.where(lane_low, even, odd)
                for a in range(2):
                    part = cjo[pl.ds(8 * g * msg + p * 18 + 2 * j + a, 8, stride=msg), :] * got
                    proj[a] = part if proj[a] is None else proj[a] + part
            for a in range(2):
                r_out[pl.ds(8 * g * width + 2 * p + a, 8, stride=width), :] = proj[a]


def body(
    n, grp_size, blocks, per, owners, msg, live, groups, obs,
    cj_in, pj_in, slot_in, point_in, pinv_in, prhs_in, cinv, crhs,
    cam_out, pt_out, ratio_out,
    cjm, pj, slot, point, pinv, prhs, right, left, quant, zs, s_out, r_in,
    cjo, sloto, hot, pull, lhs, s_in, r_out, xs, inv, rhs, kept, final, fin, mine, sums,
    load, slot_s, slot_r, jac_s, jac_r, s_s, s_r, r_s, r_r, f_s, f_r, q_s, q_r,
):
    me = lax.axis_index("pts") * grp_size + lax.axis_index("grp")
    width = 2 * per
    is_owner = me < owners

    def at(other):
        return (other // grp_size, lax.rem(other, grp_size))

    def others(step):
        def run(k, carry):
            step(jnp.bitwise_xor(me, n - k))
            return carry

        lax.fori_loop(1, n, run, 0)

    barrier = pltpu.get_barrier_semaphore()
    others(lambda d: pl.semaphore_signal(barrier, inc=1, device_id=at(d), device_id_type=MESH))

    def loads(q):
        cols = pl.ds(pl.multiple_of((me * width + q) * 128, 128), 128)
        return (
            pltpu.make_async_copy(cinv.at[:, :, cols], inv.at[q], load.at[2 * q]),
            pltpu.make_async_copy(crhs.at[:, cols], rhs.at[q], load.at[2 * q + 1]),
        )

    for q in range(width):
        @pl.when(me * width + q < blocks)
        def _():
            for copy in loads(q):
                copy.start()

        @pl.when(me * width + q >= blocks)
        def _():
            inv[q] = jnp.zeros((9, 9, 128), F32)
            rhs[q] = jnp.zeros((9, 128), F32)

    prepare(obs, live, per, msg, cj_in, pj_in, slot_in, point_in, cjm, pj, slot, point)

    def rows(ref, index, count):
        return ref.at[pl.ds(index * count, count)]

    def send(src, src_at, dst, dst_at, count, send_sem, recv_sem, device):
        return pltpu.make_async_remote_copy(
            src_ref=rows(src, src_at, count), dst_ref=rows(dst, dst_at, count),
            send_sem=send_sem, recv_sem=recv_sem, device_id=at(device), device_id_type=MESH,
        )

    def wait_sent(src, count, send_sem, recv_sem):
        part = src.at[pl.ds(0, count)]
        pltpu.make_async_remote_copy(
            src_ref=part, dst_ref=part, send_sem=send_sem, recv_sem=recv_sem, device_id=at(me), device_id_type=MESH
        ).wait_send()

    def wait_got(dst, count, send_sem, recv_sem):
        part = dst.at[pl.ds(0, count)]
        pltpu.make_async_remote_copy(
            src_ref=part, dst_ref=part, send_sem=send_sem, recv_sem=recv_sem, device_id=at(me), device_id_type=MESH
        ).wait_recv()

    def keep(src, src_at, dst, dst_at, count):
        for k in range(count):
            dst[pl.ds(dst_at * count + k, 1), :] = src[pl.ds(src_at * count + k, 1), :]

    def to_owners(make):
        others(lambda d: pl.when(d < owners)(lambda: make(d).start()))

    def by_role(step):
        pl.when(is_owner)(lambda: step(owners - 1))
        pl.when(jnp.logical_not(is_owner))(lambda: step(owners))

    pl.semaphore_wait(barrier, n - 1)
    to_owners(lambda d: send(slot, d, sloto, me, per, slot_s, slot_r, d))
    to_owners(lambda d: send(cjm, d, cjo, me, msg, jac_s, jac_r, d))
    prepare_points(live, pinv_in, prhs_in, point, pinv, prhs, right)
    zs[...] = prhs[...]
    kept[...] = jnp.zeros_like(kept)
    pull[...] = jnp.zeros_like(pull)
    final[...] = jnp.zeros_like(final)
    r_in[...] = jnp.zeros_like(r_in)
    for q in range(width):
        @pl.when(me * width + q < blocks)
        def _():
            for copy in loads(q):
                copy.wait()

    @pl.when(is_owner)
    def _():
        keep(slot, me, sloto, me, per)
        keep(cjm, me, cjo, me, msg)
        wait_got(sloto, (n - 1) * per, slot_s, slot_r)
        build_hot(n, per, sloto, hot)

    def term(index, carry):
        zs[...] = point_solve(pinv, zs[...])
        from_points(groups, zs, pj, point, s_out)
        to_owners(lambda d: send(s_out, d, s_in, me, width, s_s, s_r, d))

        @pl.when(is_owner)
        def _():
            keep(s_out, me, s_in, me, width)

            @pl.when(index == 0)
            def _():
                wait_got(cjo, (n - 1) * msg, jac_s, jac_r)

            wait_got(s_in, (n - 1) * width, s_s, s_r)
            sums = gather_blocks(n, per, msg, s_in, cjo, hot, pull, lhs)
            for q in range(width):
                total = jnp.where(index == 0, rhs[q] - sums[q], sums[q])
                piece = None
                for j in range(9):
                    part = inv[q, j] * total[j : j + 1, :]
                    piece = part if piece is None else piece + part
                step = kept[q] + piece
                kept[q] = step
                final[9 * q : 9 * q + 9, :] = step
                xs[16 * q : 16 * q + 9, :] = jnp.where(index == TERMS, step, piece)
            spread_blocks(n, per, msg, xs, sloto, cjo, r_out)
            others(lambda d: send(r_out, d, r_in, me, width, r_s, r_r, d).start())
            keep(r_out, me, r_in, me, width)

        by_role(lambda count: wait_got(r_in, count * width, r_s, r_r))
        zs[...] = onto_points(live, groups, r_in, pj, point, quant, left, right)
        by_role(lambda count: wait_sent(s_out, count * width, s_s, s_r))
        pl.when(is_owner)(lambda: wait_sent(r_out, (n - 1) * width, r_s, r_r))
        return carry

    lax.fori_loop(0, TERMS + 1, term, 0)

    @pl.when(is_owner)
    def _():
        others(lambda d: send(final, 0, fin, me, msg, f_s, f_r, d).start())
        for k in range(msg // 8):
            fin[pl.ds(pl.multiple_of(me * msg + 8 * k, 8), 8), :] = final[8 * k : 8 * k + 8, :]

    rhs_pts = prhs[...]
    resid = rhs_pts - zs[...]
    for row, vals in ((0, resid * resid), (1, rhs_pts * rhs_pts)):
        mine[row : row + 1, :] = jnp.sum(vals, axis=0, keepdims=True)
    others(lambda d: send(mine, 0, sums, me, 2, q_s, q_r, d).start())
    keep(mine, 0, sums, me, 2)
    zs[...] = point_solve(pinv, resid)
    for s in range(16):
        pt_out[:, s * 128 : s * 128 + 128] = zs[pl.ds(s, 3, stride=16), :]
    by_role(lambda count: wait_sent(slot, count * per, slot_s, slot_r))
    by_role(lambda count: wait_sent(cjm, count * msg, jac_s, jac_r))
    wait_got(sums, (n - 1) * 2, q_s, q_r)
    total = sums[0:8, :]
    for k in range(1, n // 4):
        total = total + sums[8 * k : 8 * k + 8, :]
    even = lax.broadcasted_iota(jnp.int32, (8, 128), 0) % 2 == 0
    top = jnp.sum(jnp.where(even, total, 0.0), keepdims=True)
    low = jnp.sum(jnp.where(even, 0.0, total), keepdims=True)
    ratio_out[...] = jnp.sqrt(top / low)
    by_role(lambda count: wait_got(fin, count * msg, f_s, f_r))
    for b in range(blocks):
        base = (b // width) * msg + (b % width) * 9
        cam_out[:, b * 128 : b * 128 + 128] = fin[base : base + 9, :]

    @pl.when(is_owner)
    def _():
        for _ in range(n - 1):
            wait_sent(final, msg, f_s, f_r)

    for _ in range(n - 1):
        wait_sent(mine, 2, q_s, q_r)


def local(pts_size, grp_size, cam_jac, pt_jac, cam_slot, obs_point, cam_inverse, pt_inverse, cam_rhs, pt_rhs):
    n = pts_size * grp_size
    obs = cam_slot.shape[0]
    cameras = cam_rhs.shape[1]
    blocks = cameras // CAM_BLK
    points = pt_rhs.shape[1]
    live = -(-obs // 128)
    per = -(-live // n)
    owners = -(-live // per)
    msg = -(-18 * per // 8) * 8
    groups = -(-live // 8)
    width = 2 * per
    assert obs == blocks * 64 and points == 2048 and n % 8 == 0 and n & (n - 1) == 0 and live <= 56

    def vmem(*shape):
        return pltpu.VMEM(shape, F32)

    dma = pltpu.SemaphoreType.DMA
    anywhere = pl.BlockSpec(memory_space=pl.ANY)
    wide = live * 128
    camera_step, point_step, ratio = pl.pallas_call(
        functools.partial(body, n, grp_size, blocks, per, owners, msg, live, groups, obs),
        out_shape=(
            jax.ShapeDtypeStruct((9, cameras), F32),
            jax.ShapeDtypeStruct((3, points), F32),
            jax.ShapeDtypeStruct((1, 1), F32),
        ),
        in_specs=[VMEM] * 6 + [anywhere] * 2,
        out_specs=(VMEM, VMEM, VMEM),
        scratch_shapes=[
            vmem(owners * msg, 128), vmem(6 * 64, 128), pltpu.VMEM((64, 128), jnp.int32),
            pltpu.VMEM((64, 128), jnp.int32), vmem(9 * 16, 128), vmem(48, 128),
            pltpu.VMEM((128, wide), BF16), pltpu.VMEM((96, wide), BF16),
            vmem(3 * 64, 128), vmem(48, 128), vmem(16 * groups, 128), vmem(16 * groups, 128),
            vmem(n * msg, 128), pltpu.VMEM((n * per, 128), jnp.int32), pltpu.VMEM((per, 128, n * 128), BF16),
            vmem(n * per * 16, 128), pltpu.VMEM((per, 64, n * 128), BF16),
            vmem(n * width, 128), vmem(n * width, 128), vmem(width * 16, 128),
            vmem(width, 9, 9, 128), vmem(width, 9, 128), vmem(width, 9, 128),
            vmem(msg, 128), vmem(owners * msg, 128), vmem(2, 128), vmem(2 * n, 128),
            dma((2 * width,)), dma, dma, dma, dma, dma, dma, dma, dma, dma, dma, dma, dma,
        ],
        compiler_params=pltpu.CompilerParams(collective_id=0, has_side_effects=True),
        name="schur",
    )(
        jnp.transpose(cam_jac, (1, 0, 2)), jnp.transpose(pt_jac, (1, 0, 2)), cam_slot, obs_point,
        pt_inverse, pt_rhs, cam_inverse, cam_rhs,
    )
    return camera_step, point_step, ratio.reshape(())


def solution(mesh):
    placed = (
        P(None, None, ("pts", "grp")),
        P(None, None, ("pts", "grp")),
        P(("pts", "grp")),
        P(("pts", "grp")),
        P(),
        P(None, None, ("pts", "grp")),
        P(),
        P(None, ("pts", "grp")),
    )
    return jax.shard_map(
        functools.partial(local, mesh.shape["pts"], mesh.shape["grp"]),
        mesh=mesh,
        in_specs=placed,
        out_specs=(P(), P(None, ("pts", "grp")), P()),
        check_vma=False,
    )
```

time: 115 us -> 90.8 us (0.79)
  Pallas kernels: 104 us -> 84.6 us
  local copies, waits for them, and re-layouts: 8.57 us -> 3.51 us
    pallas_call x1, Pallas kernels: 104 us -> 84.6 us  [local(): pl.pallas_call(functools.partial(body, n, grp_size, blocks, per, owners,...]
    unnamed x4 -> x2, local copies, waits for them, and re-layouts: 7.19 us -> 3.51 us
    reshape x1 -> x0, local copies, waits for them, and re-layouts: 1.39 us -> none  [pad_obs(): return jnp.pad(v, (0, 64 * 128 - obs)).reshape(64, 128)]
where the time goes in v1:
time: 90.8 us; the launch traced here: 90.5 us
  Pallas kernels  84.6 us (93%)
  local copies, waits for them, and re-layouts  3.51 us (4%)
  between operations  2.44 us (3%)
    pallas_call x1, Pallas kernels, local(): pl.pallas_call(functools.partial(body, n, grp_size, blocks, per, owners,...  84.6 us
    unnamed x2, local copies, waits for them, and re-layouts  3.51 us

profile of v1, /device:TPU:0, one launch (start us, length us, event | category | flops | bytes accessed | tf_op | source)
XLA Modules:
  0.0 90.5 jit_solution(7043625116813186946)
XLA Ops:
  0.6 84.6 %schur.1 = (f32[9,13696]{1,0:T(8,128)}, f32[3,2048]{1,0:T(4,128)}, f32[1,1]{1,0:T(1,128)}) custom-call(f32[9,2,6848]{2,1,0:T(2,128)} %bitcast.3, f32[3,2,6848]{2,1,0:T(2,128)} %bitcast.4, s32[6848]{0:T(1024)} %slot_in.1, s32[6848]{0:T(1024)} %point_in.1, f32[3,3,2048]{2,1,0:T(4,128)} %pinv_in.1, f32[3,2048]{1,0:T(4,128)} %prhs_in.1, f32[9,9,13696]{2,1,0:T(8,128)} %cinv.1, ...), custom_call_target="tpu_custom_call" | custom-call | tf_op jit(solution)/shard_map/schur/pallas_call | solution.py:357
  85.2 2.1 %copy.14 = f32[9,13696]{1,0:T(8,128)} copy(f32[9,13696]{1,0:T(8,128)} %get-tuple-element.12) | data formatting | bytes 986112
  87.3 1.4 %copy.15 = f32[3,2048]{1,0:T(4,128)} copy(f32[3,2048]{1,0:T(4,128)} %get-tuple-element.13) | data formatting | bytes 49152
